TPU v7x, 32 devices: a whole 2x2x4 slice. The times are simulated.
32 devices in a mesh: tp: 8 (over z, y), kv: 4 (over x, core).
Axes of the slice: x: 2, y: 2, z: 4, core: 2. Of those that a mesh axis runs over, the one named last changes fastest.
Arguments:
- hidden_in: bfloat16 [2048, 4096], P(('kv', 'tp')), may hold values from -6 to 6
- gain_attn: float32 [4096], replicated, may hold values from 0.4 to 1.6
- w_qkv: bfloat16 [4096, 32, 384], P(None, 'tp'), may hold values from -0.09375 to 0.09375
- cache_kv: bfloat16 [2, 8192, 32, 256], P(None, 'kv', 'tp'), may hold values from -110 to 110
- cache_len: int32 [2], replicated, may hold values from 128 to 8192, as said below
- w_out: bfloat16 [4096, 4096], P('tp'), may hold values from -0.1875 to 0.1875
- gain_mlp: float32 [4096], replicated, may hold values from 0.1 to 1.9
- w_gate_up: bfloat16 [4096, 2, 11008], P('kv', None, 'tp'), may hold values from -0.09375 to 0.09375
- w_down: bfloat16 [11008, 4096], P('tp', 'kv'), may hold values from -0.0546875 to 0.0546875
Outputs:
- layer_out: bfloat16 [2048, 4096], P(('kv', 'tp'))
Inputs may be any that keep to these rules, and one draw needn't show every extreme that they name: `cache_len`: every length is a multiple of 128; some sequence uses the whole cache.
All inputs are finite; a program needn't handle non-finite values.
Results may differ from a plain program's by a relative error of at most 0.019.
The roundings to bfloat16 on the way count: a program that leaves them out, or rounds other values in their place, can miss the bound.
Values may be sent and summed in bfloat16 or wider, within the bound.
A program may use at most 192 MiB of HBM per device.

v0:
```python
import math
import jax
import jax.numpy as jnp
from jax import lax
from jax.sharding import PartitionSpec as P

EPSILON = 1e-05
MASKED = -1e30


def rms_scale(values_in, gain_vector):
    widened = values_in.astype(jnp.float32)
    mean_square = jnp.mean(widened * widened, axis=-1, keepdims=True)
    return (widened * lax.rsqrt(mean_square + EPSILON) * gain_vector).astype(jnp.bfloat16)


def per_device(
    hidden_in, gain_attn, w_qkv, cache_kv, cache_len, w_out, gain_mlp, w_gate_up, w_down
):
    local_heads = w_qkv.shape[1]
    head_dim = w_qkv.shape[2] // 3
    own_rows = hidden_in.shape[0]
    block_input = lax.all_gather(hidden_in, "tp", axis=0, tiled=True)
    block_rows = block_input.shape[0]
    normed = rms_scale(block_input, gain_attn)
    flat_qkv = w_qkv.reshape(w_qkv.shape[0], local_heads * 3 * head_dim)
    packed = jnp.dot(normed, flat_qkv, preferred_element_type=jnp.float32).astype(jnp.bfloat16)
    packed = packed.reshape(block_rows, local_heads, 3 * head_dim)
    key_mine = packed[:, :, head_dim : 2 * head_dim]
    value_mine = packed[:, :, 2 * head_dim :]
    query_rows = lax.all_gather(packed[:, :, :head_dim], "kv", axis=0, tiled=True)
    seq_count = cache_kv.shape[0]
    span_len = query_rows.shape[0] // seq_count
    kv_index = lax.axis_index("kv")
    cache_rows = cache_kv.shape[1]
    cache_pos = kv_index * cache_rows + jnp.arange(cache_rows, dtype=jnp.int32)
    own_seq = (kv_index * block_rows + jnp.arange(block_rows, dtype=jnp.int32)) // span_len
    row_peaks, masses, accums = ([], [], [])
    for seq_id in range(seq_count):
        query_block = query_rows[seq_id * span_len : (seq_id + 1) * span_len]
        joined_key_rows = jnp.concatenate([cache_kv[seq_id, :, :, :head_dim], key_mine], axis=0)
        joined_value_rows = jnp.concatenate([cache_kv[seq_id, :, :, head_dim:], value_mine], axis=0)
        usable = jnp.concatenate([cache_pos < cache_len[seq_id], own_seq == seq_id])
        logit_scores = jnp.einsum(
            "qhd,khd->hqk", query_block, joined_key_rows, preferred_element_type=jnp.float32
        ) / math.sqrt(head_dim)
        logit_scores = jnp.where(usable[None, None, :], logit_scores, MASKED)
        row_peak = jnp.max(logit_scores, axis=2)
        raw_weights = jnp.where(
            usable[None, None, :], jnp.exp(logit_scores - row_peak[:, :, None]), 0.0
        )
        row_peaks.append(row_peak.T)
        masses.append(jnp.sum(raw_weights, axis=2).T)
        accums.append(
            jnp.einsum(
                "hqk,khd->qhd",
                raw_weights.astype(jnp.bfloat16),
                joined_value_rows,
                preferred_element_type=jnp.float32,
            )
        )
    peak_all = jnp.concatenate(row_peaks, axis=0)
    mass_all = jnp.concatenate(masses, axis=0)
    accum_all = jnp.concatenate(accums, axis=0)
    peak_set, mass_set, accum_set = (
        lax.all_to_all(peak_all[None], "kv", split_axis=1, concat_axis=0, tiled=True),
        lax.all_to_all(mass_all[None], "kv", split_axis=1, concat_axis=0, tiled=True),
        lax.all_to_all(accum_all[None], "kv", split_axis=1, concat_axis=0, tiled=True),
    )
    peak_best = jnp.max(peak_set, axis=0)
    scaling = jnp.exp(peak_set - peak_best[None])
    mass_own = jnp.sum(mass_set * scaling, axis=0)
    accum_own = jnp.sum(accum_set * scaling[..., None], axis=0)
    attended = (
        (accum_own / mass_own[..., None])
        .astype(jnp.bfloat16)
        .reshape(block_rows, local_heads * head_dim)
    )
    tp_index = lax.axis_index("tp")
    heads_sum = lax.psum(
        jnp.dot(attended, w_out, preferred_element_type=jnp.float32).astype(jnp.bfloat16), "tp"
    ).astype(jnp.float32)
    residual = block_input.astype(jnp.float32) + heads_sum
    mlp_in = rms_scale(residual, gain_mlp)
    residual_own = lax.dynamic_slice_in_dim(residual, tp_index * own_rows, own_rows, 0)
    gate_up = jnp.einsum(
        "td,dgf->tgf",
        mlp_in,
        lax.all_gather(w_gate_up, "kv", axis=0, tiled=True),
        preferred_element_type=jnp.float32,
    )
    activated = (jax.nn.silu(gate_up[:, 0, :]) * gate_up[:, 1, :]).astype(jnp.bfloat16)
    down_terms = jnp.dot(
        activated,
        lax.all_gather(w_down, "kv", axis=1, tiled=True),
        preferred_element_type=jnp.float32,
    )
    down_own = lax.psum_scatter(
        down_terms.astype(jnp.bfloat16), "tp", scatter_dimension=0, tiled=True
    ).astype(jnp.float32)
    return (residual_own + down_own).astype(jnp.bfloat16)


def solution(mesh):
    in_specs = (
        P(("kv", "tp"), None),
        P(),
        P(None, "tp", None),
        P(None, "kv", "tp", None),
        P(),
        P("tp", None),
        P(),
        P("kv", None, "tp"),
        P("tp", "kv"),
    )
    out_specs = P(("kv", "tp"), None)
    return jax.shard_map(
        per_device, mesh=mesh, in_specs=in_specs, out_specs=out_specs, check_vma=False
    )
```

profile of v0, /device:TPU:0, one launch (start us, length us, event | category | flops | bytes accessed | tf_op | source)
XLA Modules:
  0.0 827.3 jit_solution(16002876231132787441)
XLA Ops:
  6.5 0.7 all-gather.5.cloned.1.call-update
  7.3 0.0 all-gather.7.cloned.1.call-start
  7.3 12.4 %copy.51 = bf16[512,8,4,384]{3,1,2,0:T(8,128)(2,1)} copy(bf16[512,8,4,384]{3,2,1,0:T(4,128)(2,1)} %bitcast.50) | data formatting | bytes 25165824
  19.7 65.3 %all-gather.5.cloned.1.call-done = bf16[512,4096]{1,0:T(8,128)(2,1)} async-done(((bf16[64,4096]{1,0:T(8,128)(2,1)}), bf16[512,4096]{1,0:T(8,128)(2,1)}) %all-gather.5.cloned.1.call-update) | async-done | bytes 4194320 | tf_op jit(solution)/shard_map/all_gather | solution.py:23
  85.0 3.1 fusion.12
  88.1 11.0 %fusion.24 = bf16[512,1536]{1,0:T(8,128)(2,1)S(1)} fusion(bf16[4096,1536]{1,0:T(8,128)(2,1)} %bitcast.51, bf16[512,4096]{1,0:T(8,128)(2,1)} %all-gather.5.cloned.1.call-done, f32[4096]{0:T(1024)S(1)} %copy-done.5, f32[512]{0:T(512)S(1)} %add_rsqrt_fusion.1), kind=kOutput, calls=%fused_computation.37 | convolution fusion | flops 6451625984 | bytes 18368512 | tf_op jit(solution)/shard_map/dot_general | solution.py:27
  99.1 0.4 reshape.57
  99.5 0.5 fusion.62
  100.0 0.9 copy.46
  100.9 0.0 all-gather.7.cloned.1.call-update
  100.9 6.4 fusion.61
  107.4 4.4 copy.44
  111.8 2.6 copy.49
  114.4 0.6 fusion.63
  115.0 1.3 fusion.45
  116.3 4.1 copy_bitcast_fusion
  120.4 1.1 copy.45
  121.5 0.1 copy.48
  121.6 0.6 all-gather.7.cloned.1.call-done
  122.2 19.7 %fusion.1 = (f32[4,1024]{1,0:T(4,128)S(1)}, f32[4,1024,2560]{2,1,0:T(8,128)}) fusion(pred[2560]{0:T(1024)(128)(4,1)S(1)} %pad_add_fusion.1, bf16[512,4,128]{2,0,1:T(8,128)(2,1)S(1)} %copy.48, bf16[2048,4,128]{2,0,1:T(8,128)(2,1)} %get-tuple-element.26, bf16[2048,4,128]{2,0,1:T(8,128)(2,1)} %all-gather.7.cloned.1.call-done), kind=kOutput, calls=%fused_computation.5 | convolution fusion | flops 2721050624 | bytes 45632000 | tf_op jit(solution)/shard_map/qhd,khd->hqk/dot_general | solution.py:44
  141.8 19.2 %fusion.4 = f32[4,1024]{1,0:T(4,128)S(1)} fusion(f32[4,1024,2560]{2,1,0:T(8,128)} %get-tuple-element.19, f32[4,1024]{1,0:T(4,128)S(1)} %get-tuple-element.18, pred[2560]{0:T(1024)(128)(4,1)S(1)} %pad_add_fusion.1), kind=kLoop, calls=%fused_computation.8 | loop fusion | flops 52424704 | bytes 41978368 | tf_op jit(solution)/shard_map/reduce_sum | solution.py:53
  161.1 17.9 %fusion.38 = f32[1024,4,128]{0,2,1:T(8,128)} fusion(f32[4,1024,2560]{2,1,0:T(8,128)} %get-tuple-element.19, f32[4,1024]{1,0:T(4,128)S(1)} %get-tuple-element.18, pred[2560]{0:T(1024)(128)(4,1)S(1)} %pad_add_fusion.1, bf16[512,4,128]{0,2,1:T(8,128)(2,1)S(1)} %copy-done.3, bf16[2048,4,128]{0,2,1:T(8,128)(2,1)S(1)} %bitcast.59), kind=kOutput, calls=%fused_computation.51 | convolution fusion | flops 2742026240 | bytes 46680576 | tf_op jit(solution)/shard_map/hqk,khd->qhd/dot_general | solution.py:55
  178.9 19.0 %fusion = (f32[4,1024]{1,0:T(4,128)S(1)}, f32[4,1024,2560]{2,1,0:T(8,128)}) fusion(pred[2560]{0:T(1024)(128)(4,1)S(1)} %pad_add_fusion, bf16[512,4,128]{2,0,1:T(8,128)(2,1)S(1)} %copy.48, bf16[2048,4,128]{2,0,1:T(8,128)(2,1)S(1)} %get-tuple-element.27, bf16[2048,4,128]{2,0,1:T(8,128)(2,1)} %all-gather.7.cloned.1.call-done), kind=kOutput, calls=%fused_computation.4 | convolution fusion | flops 2721050624 | bytes 45632000 | tf_op jit(solution)/shard_map/qhd,khd->hqk/dot_general | solution.py:44
  198.0 19.2 %fusion.2 = f32[4,1024]{1,0:T(4,128)S(1)} fusion(f32[4,1024,2560]{2,1,0:T(8,128)} %get-tuple-element.21, f32[4,1024]{1,0:T(4,128)S(1)} %get-tuple-element.20, pred[2560]{0:T(1024)(128)(4,1)S(1)} %pad_add_fusion), kind=kLoop, calls=%fused_computation.6 | loop fusion | flops 52424704 | bytes 41978368 | tf_op jit(solution)/shard_map/reduce_sum | solution.py:53
  217.2 17.9 %fusion.35 = f32[1024,4,128]{0,2,1:T(8,128)} fusion(f32[4,1024,2560]{2,1,0:T(8,128)} %get-tuple-element.21, f32[4,1024]{1,0:T(4,128)S(1)} %get-tuple-element.20, pred[2560]{0:T(1024)(128)(4,1)S(1)} %pad_add_fusion, bf16[512,4,128]{0,2,1:T(8,128)(2,1)S(1)} %copy-done.3, bf16[2048,4,128]{0,2,1:T(8,128)(2,1)S(1)} %bitcast.58), kind=kOutput, calls=%fused_computation.50 | convolution fusion | flops 2742026240 | bytes 46680576 | tf_op jit(solution)/shard_map/hqk,khd->qhd/dot_general | solution.py:55
  235.1 0.4 copy.38
  235.5 0.6 broadcast.98
  236.1 9.5 %reduce.2 = f32[2048,4]{1,0:T(8,128)S(1)} reduce(f32[2048,1,4]{2,1,0:T(1,128)S(1)} %bitcast.54, f32[]{:T(128)} %broadcast.98), dimensions={1}, to_apply=%bitcast.41.reduce_sub_computation | reduce | bytes 65540
  245.6 1.3 reshape.59
  247.0 3.3 all-to-all-start.1
  250.3 0.4 copy.42
  250.6 9.3 %reduce = f32[2048,4]{1,0:T(8,128)S(1)} reduce(f32[2048,1,4]{2,1,0:T(1,128)S(1)} %bitcast.55, f32[]{:T(128)} %broadcast.98), dimensions={1}, to_apply=%bitcast.43.reduce_sub_computation | reduce | bytes 65540
  260.0 1.4 reshape.61
  261.3 3.3 all-to-all-start.2
  264.6 4.6 maximum_bitcast_fusion
  269.2 5.2 copy.37
  274.5 4.9 all-to-all-start
  279.3 0.4 all-reduce.2.cloned.1.call-start
  279.8 0.7 reduce.3
  280.5 1.7 reshape.60
  282.2 0.3 copy.40
  282.5 0.1 reduce_max.29
  282.6 0.1 copy.39
  282.7 0.7 reduce.1
  283.5 1.7 reshape.62
  285.1 0.3 copy.43
  285.5 42.0 %all-to-all-done = f32[1,2048,4,128]{3,2,0,1:T(4,128)} async-done(((f32[1,2048,4,128]{3,2,0,1:T(4,128)}), f32[1,2048,4,128]{3,2,0,1:T(4,128)}, u32[]{:S(2)}, u32[]{:S(2)}) %all-to-all-start) | async-done | bytes 4194336 | tf_op jit(solution)/shard_map/all_to_all | solution.py:68
  327.5 5.3 copy.41
  332.9 5.1 multiply_reduce_fusion.1
  338.0 0.1 divide_convert_fusion
  338.1 4.5 convolution_convert_fusion.1
  342.7 0.0 all-gather.9.cloned.1.call-start
  342.7 0.5 all-gather.9.cloned.1.call-update
  343.2 0.0 all-gather.11.cloned.1.call-start
  343.3 0.5 all-gather.11.cloned.1.call-update
  343.8 0.2 reduce-scatter.2.cloned.1.call-start
  344.1 155.1 %all-reduce.2.cloned.1.call-done = bf16[512,4096]{1,0:T(8,128)(2,1)} async-done(((bf16[512,4096]{1,0:T(8,128)(2,1)}), bf16[512,4096]{1,0:T(8,128)(2,1)}) %all-reduce.2.cloned.1.call-update) | async-done | bytes 4194320 | tf_op jit(solution)/shard_map/psum | solution.py:80
  499.2 9.2 %convert_add_fusion = (f32[512,4096]{1,0:T(8,128)}, f32[512]{0:T(512)S(1)}) fusion(bf16[512,4096]{1,0:T(8,128)(2,1)} %all-gather.5.cloned.1.call-done, bf16[512,4096]{1,0:T(8,128)(2,1)} %all-reduce.2.cloned.1.call-done), kind=kLoop, calls=%fused_computation.14 | loop fusion | flops 10485248 | bytes 16779264 | tf_op jit(solution)/shard_map/add | solution.py:83
  508.4 131.6 %all-gather.9.cloned.1.call-done = bf16[4096,2,1376]{0,2,1:T(8,128)(2,1)} async-done(((bf16[1024,2,1376]{0,2,1:T(8,128)(2,1)}), bf16[4096,2,1376]{0,2,1:T(8,128)(2,1)}) %all-gather.9.cloned.1.call-update) | async-done | bytes 22544400 | tf_op jit(solution)/shard_map/all_gather | solution.py:89
  639.9 20.5 %fusion.16 = f32[512,2,1376]{0,2,1:T(8,128)} fusion(bf16[4096,2,1376]{0,2,1:T(8,128)(2,1)} %all-gather.9.cloned.1.call-done, f32[4096]{0:T(1024)S(1)} %copy-done.6, f32[512]{0:T(512)S(1)} %add_rsqrt_fusion, bf16[512,4096]{1,0:T(8,128)(2,1)} %all-gather.5.cloned.1.call-done, bf16[512,4096]{1,0:T(8,128)(2,1)} %all-reduce.2.cloned.1.call-done), kind=kOutput, calls=%fused_computation.25 | convolution fusion | flops 11555307520 | bytes 36587520 | tf_op jit(solution)/shard_map/td,dgf->tgf/dot_general | solution.py:86
  660.4 55.6 %all-gather.11.cloned.1.call-done = bf16[1376,4096]{1,0:T(8,128)(2,1)} async-done(((bf16[1376,1024]{1,0:T(8,128)(2,1)}), bf16[1376,4096]{1,0:T(8,128)(2,1)}) %all-gather.11.cloned.1.call-update) | async-done | bytes 11272208 | tf_op jit(solution)/shard_map/all_gather | solution.py:95
  716.0 13.6 %convolution_convert_fusion = bf16[512,4096]{1,0:T(8,128)(2,1)} fusion(bf16[1376,4096]{1,0:T(8,128)(2,1)} %all-gather.11.cloned.1.call-done, f32[512,2,1376]{0,2,1:T(8,128)} %fusion.16), kind=kOutput, calls=%fused_computation.22 | convolution fusion | flops 5777686528 | bytes 21102592 | tf_op jit(solution)/shard_map/dot_general | solution.py:93
  729.6 88.4 %reduce-scatter.2.cloned.1.call-done = bf16[64,4096]{1,0:T(8,128)(2,1)} async-done(((bf16[512,4096]{1,0:T(8,128)(2,1)}), bf16[64,4096]{1,0:T(8,128)(2,1)}) %reduce-scatter.2.cloned.1.call-update) | async-done | bytes 524304 | tf_op jit(solution)/shard_map/reduce_scatter | solution.py:98
  818.0 2.3 add_convert_fusion
  (27 shorter events, 0.2 us)
Async XLA Ops:
  6.5 78.5 %all-gather.5.cloned.1.call-start = ((), (), s32[]{:S(2)}) async-start(), calls=%async_computation.4 | async-start | bytes 4718592 | tf_op jit(solution)/shard_map/all_gather | solution.py:23
  7.3 114.9 %all-gather.7.cloned.1.call-start = ((), (), s32[]{:S(2)}) async-start(), calls=%async_computation.5 | async-start | bytes 2621440 | tf_op jit(solution)/shard_map/all_gather | solution.py:31
  7.3 80.8 %copy-start.5 = (f32[4096]{0:T(1024)S(1)}, f32[4096]{0:T(1024)}, u32[]{:S(2)}) copy-start(f32[4096]{0:T(1024)} %param.10) | copy-start | bytes 49156
  107.4 7.1 copy-start.4
  141.8 19.2 %copy-start.2 = (bf16[1,2048,4,128]{1,3,2,0:T(8,128)(2,1)S(1)}, bf16[1,2048,4,128]{1,3,2,0:T(8,128)(2,1)}, u32[]{:S(2)}) copy-start(bf16[1,2048,4,128]{1,3,2,0:T(8,128)(2,1)} %copy.49) | copy-start | bytes 6291460
  141.8 19.2 %copy-start.3 = (bf16[512,4,128]{0,2,1:T(8,128)(2,1)S(1)}, bf16[512,4,128]{0,2,1:T(8,128)(2,1)}, u32[]{:S(2)}) copy-start(bf16[512,4,128]{0,2,1:T(8,128)(2,1)} %copy.45) | copy-start | bytes 1572868
  198.0 19.2 %copy-start.1 = (bf16[1,2048,4,128]{1,3,2,0:T(8,128)(2,1)S(1)}, bf16[1,2048,4,128]{1,3,2,0:T(8,128)(2,1)}, u32[]{:S(2)}) copy-start(bf16[1,2048,4,128]{1,3,2,0:T(8,128)(2,1)} %copy.44) | copy-start | bytes 6291460
  247.0 14.4 %all-to-all-start.1 = ((f32[4,1,2048]{2,1,0:T(1,128)}), f32[4,1,2048]{2,1,0:T(1,128)S(1)}, u32[]{:S(2)}, u32[]{:S(2)}) async-start(f32[4,1,2048]{2,1,0:T(1,128)} %reshape.59), calls=%async_computation.1 | async-start | bytes 65536 | tf_op jit(solution)/shard_map/all_to_all | solution.py:66
  261.3 13.2 %all-to-all-start.2 = ((f32[4,1,2048]{2,1,0:T(1,128)}), f32[4,1,2048]{2,1,0:T(1,128)S(1)}, u32[]{:S(2)}, u32[]{:S(2)}) async-start(f32[4,1,2048]{2,1,0:T(1,128)} %reshape.61), calls=%async_computation.2 | async-start | bytes 65536 | tf_op jit(solution)/shard_map/all_to_all | solution.py:67
  274.5 53.1 %all-to-all-start = ((f32[1,2048,4,128]{3,2,0,1:T(4,128)}), f32[1,2048,4,128]{3,2,0,1:T(4,128)}, u32[]{:S(2)}, u32[]{:S(2)}) async-start(f32[1,2048,4,128]{3,2,0,1:T(4,128)} %copy.37), calls=%async_computation | async-start | bytes 8388608 | tf_op jit(solution)/shard_map/all_to_all | solution.py:68
  279.3 219.8 %all-reduce.2.cloned.1.call-start = ((), (), s32[]{:S(2)}) async-start(), calls=%async_computation.6 | async-start | bytes 8388608 | tf_op jit(solution)/shard_map/psum | solution.py:80
  332.9 5.3 copy-start
  342.7 297.3 %all-gather.9.cloned.1.call-start = ((), (), s32[]{:S(2)}) async-start(), calls=%async_computation.7 | async-start | bytes 28180480 | tf_op jit(solution)/shard_map/all_gather | solution.py:89
  343.2 372.8 %all-gather.11.cloned.1.call-start = ((), (), s32[]{:S(2)}) async-start(), calls=%async_computation.8 | async-start | bytes 14090240 | tf_op jit(solution)/shard_map/all_gather | solution.py:95
  343.8 296.1 %copy-start.6 = (f32[4096]{0:T(1024)S(1)}, f32[4096]{0:T(1024)}, u32[]{:S(2)}) copy-start(f32[4096]{0:T(1024)} %param.15) | copy-start | bytes 49156
  343.8 474.2 %reduce-scatter.2.cloned.1.call-start = ((), (), s32[]{:S(2)}) async-start(), calls=%async_computation.9 | async-start | bytes 4718592 | tf_op jit(solution)/shard_map/reduce_scatter | solution.py:98
Sparse Core Ops, SparseCore 0:
  9.5 75.5 all-gather.4
  101.0 21.0 all-gather.6
  342.8 156.3 all-reduce.1
  500.6 139.2 all-gather.8
  641.3 74.6 all-gather.10
  729.7 88.2 reduce-scatter.1
where the time goes:
time: 835 us; the launch traced here: 827 us
  waiting for transfers between devices  540 us (65%)
  matrix products  124 us (15%)
  other arithmetic  84.6 us (10%)
  local copies, waits for them, and re-layouts  52.2 us (6%)
  between operations  13.9 us (2%)
  starting transfers between devices  12.2 us (1%)
    psum x1, waiting for transfers between devices, per_device(): lax.psum(jnp.dot(attended, w_out, preferred_element_type=jnp.float32).ast...  155 us
    all_gather x1, waiting for transfers between devices, per_device(): lax.all_gather(w_gate_up, 'kv', axis=0, tiled=True)  132 us
    reduce_scatter x1, waiting for transfers between devices, per_device(): lax.psum_scatter(down_terms.astype(jnp.bfloat16), 'tp', scatter_dimension...  88.4 us
    all_gather x1, waiting for transfers between devices, per_device(): block_input = lax.all_gather(hidden_in, 'tp', axis=0, tiled=True)  65.3 us
    all_gather x1, waiting for transfers between devices, per_device(): lax.all_gather(w_down, 'kv', axis=1, tiled=True)  55.6 us
    all_to_all x1, waiting for transfers between devices, per_device(): lax.all_to_all(accum_all[None], 'kv', split_axis=1, concat_axis=0, tiled=...  42 us
    dot_general x2, matrix products, per_device(): jnp.einsum('qhd,khd->hqk', query_block, joined_key_rows, preferred_elemen...  38.7 us
    reduce_sum x2, other arithmetic, per_device(): masses.append(jnp.sum(raw_weights, axis=2).T)  38.4 us
  transfers between devices with their start and end apart: 9, of which 7 were waited for; matrix products, arithmetic and copies ran while one was open for 11% of the time, Pallas kernels for 0%

commit v1 on v0

--- a/solution.py
+++ b/solution.py
@@ -6,6 +6,12 @@
 
 EPSILON = 1e-05
 MASKED = -1e30
+
+
+def all_parts(shard, axis, d):
+    pieces = lax.all_gather(shard, axis, axis=0, tiled=False)
+    out = jnp.concatenate(pieces, axis=d)
+    return out
 
 
 def rms_scale(values_in, gain_vector):
@@ -90,11 +96,7 @@
         preferred_element_type=jnp.float32,
     )
     activated = (jax.nn.silu(gate_up[:, 0, :]) * gate_up[:, 1, :]).astype(jnp.bfloat16)
-    down_terms = jnp.dot(
-        activated,
-        lax.all_gather(w_down, "kv", axis=1, tiled=True),
-        preferred_element_type=jnp.float32,
-    )
+    down_terms = jnp.dot(activated, all_parts(w_down, "kv", 1), preferred_element_type=jnp.float32)
     down_own = lax.psum_scatter(
         down_terms.astype(jnp.bfloat16), "tp", scatter_dimension=0, tiled=True
     ).astype(jnp.float32)

time: 835 us -> 778 us (0.932)
  waiting for transfers between devices: 540 us -> 470 us
  local copies, waits for them, and re-layouts: 52.2 us -> 67.9 us
    all_gather x1, waiting for transfers between devices: 55.6 us -> 0.02 us  [all_parts(): pieces = lax.all_gather(shard, axis, axis=0, tiled=False)]
    all_gather x0 -> x1, local copies, waits for them, and re-layouts: none -> 15.6 us  [all_parts(): pieces = lax.all_gather(shard, axis, axis=0, tiled=False)]
    psum x1, waiting for transfers between devices: 155 us -> 140 us  [per_device(): lax.psum(jnp.dot(attended, w_out, preferred_element_type=jnp.float32).ast...]
    unnamed x25 -> x23, local copies, waits for them, and re-layouts: 28.1 us -> 28.1 us
  transfers between devices with their start and end apart: 9 -> 9, of which waited for: 7 -> 5; matrix products, arithmetic and copies ran while one was open for 11% -> 29% of each run, Pallas kernels for 0% -> 0%
where the time goes in v1:
time: 778 us; the launch traced here: 772 us
  waiting for transfers between devices  470 us (60%)
  matrix products  125 us (16%)
  other arithmetic  84 us (11%)
  local copies, waits for them, and re-layouts  67.9 us (9%)
  between operations  14 us (2%)
  starting transfers between devices  11.6 us (1%)
    psum x1, waiting for transfers between devices, per_device(): lax.psum(jnp.dot(attended, w_out, preferred_element_type=jnp.float32).ast...  140 us
    all_gather x1, waiting for transfers between devices, per_device(): lax.all_gather(w_gate_up, 'kv', axis=0, tiled=True)  132 us
    reduce_scatter x1, waiting for transfers between devices, per_device(): lax.psum_scatter(down_terms.astype(jnp.bfloat16), 'tp', scatter_dimension...  88.4 us
    all_gather x1, waiting for transfers between devices, per_device(): block_input = lax.all_gather(hidden_in, 'tp', axis=0, tiled=True)  65.3 us
    all_to_all x1, waiting for transfers between devices, per_device(): lax.all_to_all(accum_all[None], 'kv', split_axis=1, concat_axis=0, tiled=...  42.6 us
    dot_general x2, matrix products, per_device(): jnp.einsum('qhd,khd->hqk', query_block, joined_key_rows, preferred_elemen...  42.4 us
    reduce_sum x2, other arithmetic, per_device(): masses.append(jnp.sum(raw_weights, axis=2).T)  38.1 us
    dot_general x2, matrix products, per_device(): jnp.einsum('hqk,khd->qhd', raw_weights.astype(jnp.bfloat16), joined_value...  36.1 us
  transfers between devices with their start and end apart: 9, of which 5 were waited for; matrix products, arithmetic and copies ran while one was open for 29% of the time, Pallas kernels for 0%

profile of v1, /device:TPU:0, one launch (start us, length us, event | category | flops | bytes accessed | tf_op | source)
XLA Modules:
  0.0 772.3 jit_solution(5645785185996065027)
XLA Ops:
  6.5 0.7 all-gather.6.cloned.1.call-update
  7.3 0.0 all-gather.8.cloned.1.call-start
  7.3 12.4 %copy.61 = bf16[512,8,4,384]{3,1,2,0:T(8,128)(2,1)} copy(bf16[512,8,4,384]{3,2,1,0:T(4,128)(2,1)} %bitcast.45) | data formatting | bytes 25165824
  19.7 65.3 %all-gather.6.cloned.1.call-done = bf16[512,4096]{1,0:T(8,128)(2,1)} async-done(((bf16[64,4096]{1,0:T(8,128)(2,1)}), bf16[512,4096]{1,0:T(8,128)(2,1)}) %all-gather.6.cloned.1.call-update) | async-done | bytes 4194320 | tf_op jit(solution)/shard_map/all_gather | solution.py:29
  85.0 3.1 fusion.12
  88.1 11.2 %fusion.24 = bf16[512,1536]{1,0:T(8,128)(2,1)S(1)} fusion(bf16[4096,1536]{1,0:T(8,128)(2,1)} %bitcast.46, bf16[512,4096]{1,0:T(8,128)(2,1)} %all-gather.6.cloned.1.call-done, f32[4096]{0:T(1024)S(1)} %copy-done.4, f32[512]{0:T(512)S(1)} %add_rsqrt_fusion.1), kind=kOutput, calls=%fused_computation.37 | convolution fusion | flops 6451625984 | bytes 18368512 | tf_op jit(solution)/shard_map/dot_general | solution.py:33
  99.3 0.4 reshape.64
  99.7 0.5 fusion.61
  100.3 0.9 copy.56
  101.2 0.0 all-gather.12.cloned.1.call-start
  101.2 0.7 all-gather.12.cloned.1.call-update
  101.9 0.6 fusion.62
  102.6 6.6 fusion.60
  109.1 4.4 copy.54
  113.5 2.7 copy.59
  116.2 1.2 fusion.44
  117.4 4.1 copy_bitcast_fusion
  121.5 1.1 copy.55
  122.7 0.1 copy.58
  122.8 0.0 all-gather.8.cloned.1.call-done
  122.8 22.9 %fusion.1 = (f32[4,1024]{1,0:T(4,128)S(1)}, f32[4,1024,2560]{2,1,0:T(8,128)}) fusion(pred[2560]{0:T(1024)(128)(4,1)S(1)} %pad_add_fusion.1, bf16[512,4,128]{2,0,1:T(8,128)(2,1)S(1)} %copy.58, bf16[2048,4,128]{2,0,1:T(8,128)(2,1)} %get-tuple-element.26, bf16[2048,4,128]{2,0,1:T(8,128)(2,1)} %all-gather.8.cloned.1.call-done), kind=kOutput, calls=%fused_computation.5 | convolution fusion | flops 2721050624 | bytes 45632000 | tf_op jit(solution)/shard_map/qhd,khd->hqk/dot_general | solution.py:50
  145.7 19.5 %fusion = (f32[4,1024]{1,0:T(4,128)S(1)}, f32[4,1024,2560]{2,1,0:T(8,128)}) fusion(pred[2560]{0:T(1024)(128)(4,1)S(1)} %pad_add_fusion, bf16[512,4,128]{2,0,1:T(8,128)(2,1)S(1)} %copy.58, bf16[2048,4,128]{2,0,1:T(8,128)(2,1)S(1)} %get-tuple-element.27, bf16[2048,4,128]{2,0,1:T(8,128)(2,1)} %all-gather.8.cloned.1.call-done), kind=kOutput, calls=%fused_computation.4 | convolution fusion | flops 2721050624 | bytes 45632000 | tf_op jit(solution)/shard_map/qhd,khd->hqk/dot_general | solution.py:50
  165.2 0.4 copy.47
  165.6 0.5 broadcast.100
  166.1 9.3 %reduce.2 = f32[2048,4]{1,0:T(8,128)S(1)} reduce(f32[2048,1,4]{2,1,0:T(1,128)S(1)} %bitcast.51, f32[]{:T(128)} %broadcast.100), dimensions={1}, to_apply=%bitcast.36.reduce_sub_computation | reduce | bytes 65540
  175.4 1.3 reshape.69
  176.7 3.3 all-to-all-start.1
  180.0 18.2 %fusion.37 = f32[1024,4,128]{0,2,1:T(8,128)} fusion(f32[4,1024,2560]{2,1,0:T(8,128)} %get-tuple-element.19, f32[4,1024]{1,0:T(4,128)S(1)} %get-tuple-element.18, pred[2560]{0:T(1024)(128)(4,1)S(1)} %pad_add_fusion.1, bf16[512,4,128]{0,2,1:T(8,128)(2,1)S(1)} %copy-done.2, bf16[2048,4,128]{0,2,1:T(8,128)(2,1)} %bitcast.56), kind=kOutput, calls=%fused_computation.49 | convolution fusion | flops 2742026240 | bytes 46680576 | tf_op jit(solution)/shard_map/hqk,khd->qhd/dot_general | solution.py:61
  198.2 17.9 %fusion.34 = f32[1024,4,128]{0,2,1:T(8,128)} fusion(f32[4,1024,2560]{2,1,0:T(8,128)} %get-tuple-element.21, f32[4,1024]{1,0:T(4,128)S(1)} %get-tuple-element.20, pred[2560]{0:T(1024)(128)(4,1)S(1)} %pad_add_fusion, bf16[512,4,128]{0,2,1:T(8,128)(2,1)S(1)} %copy-done.2, bf16[2048,4,128]{0,2,1:T(8,128)(2,1)S(1)} %bitcast.55), kind=kOutput, calls=%fused_computation.48 | convolution fusion | flops 2742026240 | bytes 46680576 | tf_op jit(solution)/shard_map/hqk,khd->qhd/dot_general | solution.py:61
  216.1 19.0 %fusion.4 = f32[4,1024]{1,0:T(4,128)S(1)} fusion(f32[4,1024,2560]{2,1,0:T(8,128)} %get-tuple-element.19, f32[4,1024]{1,0:T(4,128)S(1)} %get-tuple-element.18, pred[2560]{0:T(1024)(128)(4,1)S(1)} %pad_add_fusion.1), kind=kLoop, calls=%fused_computation.8 | loop fusion | flops 52424704 | bytes 41978368 | tf_op jit(solution)/shard_map/reduce_sum | solution.py:59
  235.2 19.1 %fusion.2 = f32[4,1024]{1,0:T(4,128)S(1)} fusion(f32[4,1024,2560]{2,1,0:T(8,128)} %get-tuple-element.21, f32[4,1024]{1,0:T(4,128)S(1)} %get-tuple-element.20, pred[2560]{0:T(1024)(128)(4,1)S(1)} %pad_add_fusion), kind=kLoop, calls=%fused_computation.6 | loop fusion | flops 52424704 | bytes 41978368 | tf_op jit(solution)/shard_map/reduce_sum | solution.py:59
  254.2 0.4 copy.51
  254.6 9.4 %reduce = f32[2048,4]{1,0:T(8,128)S(1)} reduce(f32[2048,1,4]{2,1,0:T(1,128)S(1)} %bitcast.52, f32[]{:T(128)} %broadcast.100), dimensions={1}, to_apply=%bitcast.38.reduce_sub_computation | reduce | bytes 65540
  264.1 1.4 reshape.71
  265.4 3.3 all-to-all-start.2
  268.7 4.6 maximum_bitcast_fusion
  273.4 5.2 copy.46
  278.6 4.9 all-to-all-start
  283.4 0.0 all-reduce.2.cloned.1.call-start
  283.5 0.7 reduce.3
  284.2 1.7 reshape.70
  285.8 0.3 copy.49
  286.1 0.1 reduce_max.29
  286.3 0.1 copy.48
  286.4 0.7 reduce.1
  287.0 1.7 reshape.72
  288.7 0.3 copy.52
  289.1 42.6 %all-to-all-done = f32[1,2048,4,128]{3,2,0,1:T(4,128)} async-done(((f32[1,2048,4,128]{3,2,0,1:T(4,128)}), f32[1,2048,4,128]{3,2,0,1:T(4,128)}, u32[]{:S(2)}, u32[]{:S(2)}) %all-to-all-start) | async-done | bytes 4194336 | tf_op jit(solution)/shard_map/all_to_all | solution.py:74
  331.6 5.3 copy.50
  337.0 5.1 multiply_reduce_fusion.1
  342.1 0.1 divide_convert_fusion
  342.2 4.5 convolution_convert_fusion.1
  346.8 0.0 all-gather.10.cloned.1.call-start
  346.8 0.5 all-gather.10.cloned.1.call-update
  347.4 0.0 reduce-scatter.2.cloned.1.call-start
  347.4 0.0 all-gather.12.cloned.1.call-done
  347.4 15.6 %copy.53 = bf16[4,1376,1024]{1,2,0:T(8,128)(2,1)} copy(bf16[4,1376,1024]{2,1,0:T(8,128)(2,1)} %bitcast.48) | data formatting | bytes 22544384 | tf_op jit(solution)/shard_map/all_gather | solution.py:12
  363.0 140.0 %all-reduce.2.cloned.1.call-done = bf16[512,4096]{1,0:T(8,128)(2,1)} async-done(((bf16[512,4096]{1,0:T(8,128)(2,1)}), bf16[512,4096]{1,0:T(8,128)(2,1)}) %all-reduce.2.cloned.1.call-update) | async-done | bytes 4194320 | tf_op jit(solution)/shard_map/psum | solution.py:86
  503.0 9.2 %convert_add_fusion = (f32[512,4096]{1,0:T(8,128)}, f32[512]{0:T(512)S(1)}) fusion(bf16[512,4096]{1,0:T(8,128)(2,1)} %all-gather.6.cloned.1.call-done, bf16[512,4096]{1,0:T(8,128)(2,1)} %all-reduce.2.cloned.1.call-done), kind=kLoop, calls=%fused_computation.14 | loop fusion | flops 10485248 | bytes 16779264 | tf_op jit(solution)/shard_map/add | solution.py:89
  512.2 131.5 %all-gather.10.cloned.1.call-done = bf16[4096,2,1376]{0,2,1:T(8,128)(2,1)} async-done(((bf16[1024,2,1376]{0,2,1:T(8,128)(2,1)}), bf16[4096,2,1376]{0,2,1:T(8,128)(2,1)}) %all-gather.10.cloned.1.call-update) | async-done | bytes 22544400 | tf_op jit(solution)/shard_map/all_gather | solution.py:95
  643.8 18.0 %fusion.16 = f32[512,2,1376]{0,2,1:T(8,128)S(1)} fusion(bf16[4096,2,1376]{0,2,1:T(8,128)(2,1)} %all-gather.10.cloned.1.call-done, f32[4096]{0:T(1024)S(1)} %copy-done.5, f32[512]{0:T(512)S(1)} %add_rsqrt_fusion, bf16[512,4096]{1,0:T(8,128)(2,1)} %all-gather.6.cloned.1.call-done, bf16[512,4096]{1,0:T(8,128)(2,1)} %all-reduce.2.cloned.1.call-done), kind=kOutput, calls=%fused_computation.25 | convolution fusion | flops 11555307520 | bytes 36587520 | tf_op jit(solution)/shard_map/td,dgf->tgf/dot_general | solution.py:92
  661.7 12.7 %convolution_convert_fusion = bf16[512,4096]{1,0:T(8,128)(2,1)} fusion(bf16[1376,4096]{0,1:T(8,128)(2,1)} %bitcast.47, f32[512,2,1376]{0,2,1:T(8,128)S(1)} %fusion.16), kind=kOutput, calls=%fused_computation.22 | convolution fusion | flops 5777686528 | bytes 21102592 | tf_op jit(solution)/shard_map/dot_general | solution.py:99
  674.5 88.4 %reduce-scatter.2.cloned.1.call-done = bf16[64,4096]{1,0:T(8,128)(2,1)} async-done(((bf16[512,4096]{1,0:T(8,128)(2,1)}), bf16[64,4096]{1,0:T(8,128)(2,1)}) %reduce-scatter.2.cloned.1.call-update) | async-done | bytes 524304 | tf_op jit(solution)/shard_map/reduce_scatter | solution.py:100
  762.9 2.3 add_convert_fusion
  (26 shorter events, 0.2 us)
Async XLA Ops:
  6.5 78.5 %all-gather.6.cloned.1.call-start = ((), (), s32[]{:S(2)}) async-start(), calls=%async_computation.4 | async-start | bytes 4718592 | tf_op jit(solution)/shard_map/all_gather | solution.py:29
  7.3 115.5 %all-gather.8.cloned.1.call-start = ((), (), s32[]{:S(2)}) async-start(), calls=%async_computation.5 | async-start | bytes 2621440 | tf_op jit(solution)/shard_map/all_gather | solution.py:37
  7.3 80.8 %copy-start.4 = (f32[4096]{0:T(1024)S(1)}, f32[4096]{0:T(1024)}, u32[]{:S(2)}) copy-start(f32[4096]{0:T(1024)} %param.10) | copy-start | bytes 49156
  99.3 2.6 copy-start.3
  101.2 246.3 %all-gather.12.cloned.1.call-start = ((), (), s32[]{:S(2)}) async-start(), calls=%async_computation.9 | async-start | bytes 14090240 | tf_op jit(solution)/shard_map/all_gather | solution.py:12
  145.7 34.3 %copy-start.2 = (bf16[512,4,128]{0,2,1:T(8,128)(2,1)S(1)}, bf16[512,4,128]{0,2,1:T(8,128)(2,1)}, u32[]{:S(2)}) copy-start(bf16[512,4,128]{0,2,1:T(8,128)(2,1)} %copy.55) | copy-start | bytes 1572868
  176.7 88.7 %all-to-all-start.1 = ((f32[4,1,2048]{2,1,0:T(1,128)}), f32[4,1,2048]{2,1,0:T(1,128)S(1)}, u32[]{:S(2)}, u32[]{:S(2)}) async-start(f32[4,1,2048]{2,1,0:T(1,128)} %reshape.69), calls=%async_computation.1 | async-start | bytes 65536 | tf_op jit(solution)/shard_map/all_to_all | solution.py:72
  180.0 18.2 %copy-start.1 = (bf16[1,2048,4,128]{1,3,2,0:T(8,128)(2,1)S(1)}, bf16[1,2048,4,128]{1,3,2,0:T(8,128)(2,1)}, u32[]{:S(2)}) copy-start(bf16[1,2048,4,128]{1,3,2,0:T(8,128)(2,1)} %copy.54) | copy-start | bytes 6291460
  265.4 13.2 %all-to-all-start.2 = ((f32[4,1,2048]{2,1,0:T(1,128)}), f32[4,1,2048]{2,1,0:T(1,128)S(1)}, u32[]{:S(2)}, u32[]{:S(2)}) async-start(f32[4,1,2048]{2,1,0:T(1,128)} %reshape.71), calls=%async_computation.2 | async-start | bytes 65536 | tf_op jit(solution)/shard_map/all_to_all | solution.py:73
  278.6 53.1 %all-to-all-start = ((f32[1,2048,4,128]{3,2,0,1:T(4,128)}), f32[1,2048,4,128]{3,2,0,1:T(4,128)}, u32[]{:S(2)}, u32[]{:S(2)}) async-start(f32[1,2048,4,128]{3,2,0,1:T(4,128)} %copy.46), calls=%async_computation | async-start | bytes 8388608 | tf_op jit(solution)/shard_map/all_to_all | solution.py:74
  283.4 219.6 %all-reduce.2.cloned.1.call-start = ((), (), s32[]{:S(2)}) async-start(), calls=%async_computation.6 | async-start | bytes 8388608 | tf_op jit(solution)/shard_map/psum | solution.py:86
  337.0 5.3 copy-start
  346.8 297.0 %all-gather.10.cloned.1.call-start = ((), (), s32[]{:S(2)}) async-start(), calls=%async_computation.7 | async-start | bytes 28180480 | tf_op jit(solution)/shard_map/all_gather | solution.py:95
  347.4 415.5 %reduce-scatter.2.cloned.1.call-start = ((), (), s32[]{:S(2)}) async-start(), calls=%async_computation.8 | async-start | bytes 4718592 | tf_op jit(solution)/shard_map/reduce_scatter | solution.py:100
  363.0 280.8 %copy-start.5 = (f32[4096]{0:T(1024)S(1)}, f32[4096]{0:T(1024)}, u32[]{:S(2)}) copy-start(f32[4096]{0:T(1024)} %param.15) | copy-start | bytes 49156
Sparse Core Ops, SparseCore 0:
  9.5 75.5 all-gather.5
  101.3 21.0 all-gather.7
  124.0 74.9 all-gather.11
  346.9 156.0 all-reduce.1
  504.4 139.2 all-gather.9
  674.6 88.2 reduce-scatter.1
